TPU v7x, 32 devices: a whole 2x2x4 slice. The times are simulated.
32 devices in a mesh: section: 4 (over y, x), expert: 8 (over z, core).
Axes of the slice: x: 2, y: 2, z: 4, core: 2. Of those that a mesh axis runs over, the one named last changes fastest.
Arguments:
- tokens: bfloat16 [8, 64, 2048], P(None, 'expert'), may hold values from -6 to 6
- norm_gain: float32 [2, 2048], replicated, may hold values from 0.1 to 1.9
- w_gate: bfloat16 [4, 2048, 14336], P('section', None, 'expert'), may hold values from -0.125 to 0.125
- w_up: bfloat16 [4, 2048, 14336], P('section', None, 'expert'), may hold values from -0.125 to 0.125
- w_down: bfloat16 [4, 14336, 2048], P('section', 'expert'), may hold values from -0.0625 to 0.0625
- expert_ids: int32 [2, 8, 64, 2], P(None, None, 'expert'), may hold values from 0 to 3, as said below
- slot_ids: int32 [2, 8, 64, 2], P(None, None, 'expert'), may hold values from 0 to 4, as said below
- dropped: int32 [2, 8, 64, 2], P(None, None, 'expert'), may hold values from 0 to 1, as said below
- gate_weights: float32 [2, 8, 64, 2], P(None, None, 'expert'), may hold values from 0.1 to 1
Outputs:
- states: bfloat16 [4, 8, 64, 2048], P('section', None, 'expert')
Inputs may be any that keep to these rules, and one draw needn't show every extreme that they name: `expert_ids`: the two experts of a token differ. `slot_ids`: among the kept choices of the tokens of one index of expert that name one expert, the slots are 0, 1, ... up to their count less one, each once. At most 5 kept choices of the tokens of one index of expert name one expert, and a choice is dropped only where 5 kept choices of its index of expert name its expert; in each layer and micro-batch some expert receives exactly 5 kept choices from every index of expert.
All inputs are finite; a program needn't handle non-finite values.
Results may differ from a plain program's by a relative error of at most 0.025.
Values may be sent and summed in bfloat16 or wider, within the bound.
No kernel may reach another device: no remote copies, remote signals or barrier semaphores. Data moves between devices by JAX's collectives and lax.ppermute only.
A program may use at most 64 MiB of HBM per device.

v0:
```python
import jax
import jax.numpy as jnp
from jax import lax
from jax.sharding import PartitionSpec as P

EXPERTS = 4


def shortened(value):
    return jax.tree.map(lambda a: a.astype(jnp.bfloat16) if a.dtype == jnp.float32 else a, value)


def shifted(value, axis, by):
    size = lax.axis_size(axis)
    pairs = [(i, i + by) for i in range(size) if 0 <= i + by < size]
    return lax.ppermute(value, axis, pairs)


def on_device(tokens, norm_gain, w_gate, w_up, w_down, expert_ids, slot_ids, dropped, gate_weights):
    groups = lax.axis_size("expert")
    sections = lax.axis_size("section")
    section_at = lax.axis_index("section")
    local_count = EXPERTS // 2
    shards = groups // local_count
    micro_count, tok_rows, model_width = tokens.shape
    capacity = 5 * tok_rows // (2 * EXPERTS)
    slot_limit = local_count * capacity
    layer_at = section_at // 2
    half_at = section_at % 2
    odd_section = half_at == 1
    gain_row = lax.dynamic_index_in_dim(norm_gain, layer_at, 0, keepdims=False)
    gate_mat = w_gate[0]
    up_mat = w_up[0]
    down_mat = w_down[0]
    route_all = lax.dynamic_index_in_dim(expert_ids, layer_at, 0, keepdims=False)
    slot_all = lax.dynamic_index_in_dim(slot_ids, layer_at, 0, keepdims=False)
    drop_all = lax.dynamic_index_in_dim(dropped, layer_at, 0, keepdims=False)
    weigh_all = lax.dynamic_index_in_dim(gate_weights, layer_at, 0, keepdims=False)

    def expert_rows(received):
        flat_rows = received.reshape(-1, model_width)
        gate_vals = jnp.dot(flat_rows, gate_mat, preferred_element_type=jnp.float32)
        up_vals = jnp.dot(flat_rows, up_mat, preferred_element_type=jnp.float32)
        hidden = (jax.nn.silu(gate_vals) * up_vals).astype(jnp.bfloat16)
        partial_rows = jnp.dot(hidden, down_mat, preferred_element_type=jnp.float32).astype(
            jnp.bfloat16
        )
        return partial_rows.reshape(received.shape)

    def skip_rows(received):
        return jnp.zeros(received.shape, jnp.bfloat16)

    def run_experts(outgoing, active):
        received = lax.all_to_all(outgoing, "expert", split_axis=0, concat_axis=0, tiled=True)
        computed = lax.cond(active, expert_rows, skip_rows, received)
        returned = lax.all_to_all(computed, "expert", split_axis=0, concat_axis=0, tiled=True)
        return returned

    def advance(tick_count, carry):
        incoming, states = carry
        micro_at = tick_count - section_at
        active = (micro_at >= 0) & (micro_at < micro_count)
        micro_index = jnp.clip(micro_at, 0, micro_count - 1)
        fresh_rows = lax.dynamic_index_in_dim(tokens, micro_index, 0, keepdims=False)
        route_now = lax.dynamic_index_in_dim(route_all, micro_index, 0, keepdims=False)
        slot_now = lax.dynamic_index_in_dim(slot_all, micro_index, 0, keepdims=False)
        drop_now = lax.dynamic_index_in_dim(drop_all, micro_index, 0, keepdims=False)
        weigh_now = lax.dynamic_index_in_dim(weigh_all, micro_index, 0, keepdims=False)
        kept_mask = drop_now == 0
        passed_state = incoming[0]
        prior_rows = [incoming[1], incoming[2]]
        current = jnp.where(section_at == 0, fresh_rows, passed_state)
        wide_rows = current.astype(jnp.float32)
        inv_scale = lax.rsqrt(jnp.mean(wide_rows * wide_rows, axis=-1, keepdims=True) + 1e-05)
        normed = (wide_rows * inv_scale * gain_row).astype(jnp.bfloat16)
        local_id = route_now - half_at * local_count
        owned = kept_mask & (local_id >= 0) & (local_id < local_count)
        target = jnp.where(owned, local_id * capacity + slot_now, slot_limit)
        buffer = jnp.zeros((slot_limit, model_width), jnp.bfloat16)
        buffer = buffer.at[target[:, 0]].set(normed, mode="drop")
        buffer = buffer.at[target[:, 1]].set(normed, mode="drop")
        buffer = buffer.reshape(local_count, capacity, model_width)
        outgoing = jnp.repeat(buffer, shards, axis=0)
        returned = run_experts(outgoing, active)
        summed = jnp.sum(
            returned.astype(jnp.float32).reshape(local_count, shards, capacity, model_width), axis=1
        )
        flat_back = summed.astype(jnp.bfloat16).reshape(slot_limit, model_width)
        clipped = jnp.minimum(target, slot_limit - 1)
        combined = wide_rows
        chosen_rows = []
        for member in range(2):
            own_rows = flat_back[clipped[:, member]]
            chosen = jnp.where(owned[:, member : member + 1], own_rows, prior_rows[member])
            chosen_rows.append(chosen)
            combined = combined + weigh_now[:, member : member + 1] * chosen.astype(jnp.float32)
        mixed_rows = combined.astype(jnp.bfloat16)
        updated = lax.dynamic_update_index_in_dim(states, mixed_rows, micro_index, 0)
        states = jnp.where(active, updated, states)
        zero_rows = jnp.zeros_like(current)
        even_load = jnp.stack([current, chosen_rows[0], chosen_rows[1]])
        odd_load = jnp.stack([mixed_rows, zero_rows, zero_rows])
        payload = jnp.where(odd_section, odd_load, even_load)
        passed = shifted(shortened(payload), "section", 1).astype(payload.dtype)
        return (passed, states)

    start_load = jnp.zeros((3, tok_rows, model_width), jnp.bfloat16)
    initial = (start_load, jnp.zeros((micro_count, tok_rows, model_width), jnp.bfloat16))
    final_load, states = lax.fori_loop(0, micro_count + sections - 1, advance, initial)
    return states[None]


def solution(mesh):
    return jax.shard_map(
        on_device,
        mesh=mesh,
        in_specs=(
            P(None, "expert", None),
            P(),
            P("section", None, "expert"),
            P("section", None, "expert"),
            P("section", "expert", None),
            P(None, None, "expert", None),
            P(None, None, "expert", None),
            P(None, None, "expert", None),
            P(None, None, "expert", None),
        ),
        out_specs=P("section", None, "expert", None),
        check_vma=False,
    )
```

profile of v0, /device:TPU:6, one launch (start us, length us, event | category | flops | bytes accessed | tf_op | source)
XLA Modules:
  0.0 560.5 jit_solution(8104722328637122049)
XLA Ops:
  2.2 557.6 %while.17 = (s32[]{:T(128)}, bf16[3,8,2048]{2,1,0:T(8,128)(2,1)S(1)}, bf16[8,8,2048]{2,1,0:T(8,128)(2,1)S(1)}, pred[]{:T(512)}, pred[]{:T(512)}, /*index=5*/s32[...) while((s32[]{:T(128)}, ...), condition=%wide.region_7.8_spmd, body=%wide.region_0.7_spmd.sunk | while | flops 881903936 | bytes 27046772 | solution.py:109
  5.5 4.9 all-to-all-start
  10.4 9.7 %all-to-all-done = bf16[8,5,2048]{2,1,0:T(8,128)(2,1)S(1)} async-done(((bf16[8,5,2048]{2,1,0:T(8,128)(2,1)}), bf16[8,5,2048]{2,1,0:T(8,128)(2,1)S(1)}, u32[]{:S(2)}, u32[]{:S(2)}) %all-to-all-start) | async-done | bytes 163872 | tf_op jit(solution)/shard_map/while/body/eval_jaxpr/all_to_all | solution.py:54
  20.8 3.4 all-to-all-start.1
  24.3 9.6 %all-to-all-done.1 = bf16[8,5,2048]{2,1,0:T(8,128)(2,1)S(1)} async-done(((bf16[8,5,2048]{2,1,0:T(8,128)(2,1)}), bf16[8,5,2048]{2,1,0:T(8,128)(2,1)S(1)}, u32[]{:S(2)}, u32[]{:S(2)}) %all-to-all-start.1) | async-done | bytes 163872 | tf_op jit(solution)/shard_map/while/body/eval_jaxpr/all_to_all | solution.py:56
  36.6 5.2 collective-permute-done
  45.0 3.4 all-to-all-start
  48.5 9.6 %all-to-all-done = bf16[8,5,2048]{2,1,0:T(8,128)(2,1)S(1)} async-done(((bf16[8,5,2048]{2,1,0:T(8,128)(2,1)}), bf16[8,5,2048]{2,1,0:T(8,128)(2,1)S(1)}, u32[]{:S(2)}, u32[]{:S(2)}) %all-to-all-start) | async-done | bytes 163872 | tf_op jit(solution)/shard_map/while/body/eval_jaxpr/all_to_all | solution.py:54
  58.8 3.4 all-to-all-start.1
  62.3 9.6 %all-to-all-done.1 = bf16[8,5,2048]{2,1,0:T(8,128)(2,1)S(1)} async-done(((bf16[8,5,2048]{2,1,0:T(8,128)(2,1)}), bf16[8,5,2048]{2,1,0:T(8,128)(2,1)S(1)}, u32[]{:S(2)}, u32[]{:S(2)}) %all-to-all-start.1) | async-done | bytes 163872 | tf_op jit(solution)/shard_map/while/body/eval_jaxpr/all_to_all | solution.py:56
  74.6 5.2 collective-permute-done
  83.0 3.4 all-to-all-start
  86.5 9.6 %all-to-all-done = bf16[8,5,2048]{2,1,0:T(8,128)(2,1)S(1)} async-done(((bf16[8,5,2048]{2,1,0:T(8,128)(2,1)}), bf16[8,5,2048]{2,1,0:T(8,128)(2,1)S(1)}, u32[]{:S(2)}, u32[]{:S(2)}) %all-to-all-start) | async-done | bytes 163872 | tf_op jit(solution)/shard_map/while/body/eval_jaxpr/all_to_all | solution.py:54
  96.8 3.4 all-to-all-start.1
  100.3 9.6 %all-to-all-done.1 = bf16[8,5,2048]{2,1,0:T(8,128)(2,1)S(1)} async-done(((bf16[8,5,2048]{2,1,0:T(8,128)(2,1)}), bf16[8,5,2048]{2,1,0:T(8,128)(2,1)S(1)}, u32[]{:S(2)}, u32[]{:S(2)}) %all-to-all-start.1) | async-done | bytes 163872 | tf_op jit(solution)/shard_map/while/body/eval_jaxpr/all_to_all | solution.py:56
  112.6 38.1 %collective-permute-done = bf16[3,8,2048]{2,1,0:T(8,128)(2,1)S(1)} collective-permute-done((bf16[3,8,2048]{2,1,0:T(8,128)(2,1)S(1)}, bf16[3,8,2048]{2,1,0:T(8,128)(2,1)S(1)}, u32[]{:S(2)}, u32[]{:S(2)}) %collective-permute-start) | collective-permute-done | bytes 98336 | tf_op jit(solution)/shard_map/while/body/eval_jaxpr/ppermute | solution.py:16
  157.4 9.6 %all-to-all-done = bf16[8,5,2048]{2,1,0:T(8,128)(2,1)S(1)} async-done(((bf16[8,5,2048]{2,1,0:T(8,128)(2,1)}), bf16[8,5,2048]{2,1,0:T(8,128)(2,1)S(1)}, u32[]{:S(2)}, u32[]{:S(2)}) %all-to-all-start) | async-done | bytes 163872 | tf_op jit(solution)/shard_map/while/body/eval_jaxpr/all_to_all | solution.py:54
  167.0 13.1 %conditional.2 = (bf16[8,5,2048]{2,1,0:T(8,128)(2,1)}) conditional(s32[]{:T(128)} %convert_element_type.138, () %tuple.73, (bf16[8,5,2048]{2,1,0:T(8,128)(2,1)S(1)}, bf16[2048,1792]{1,0:T(8,128)(2,1)}, bf16[2048,1792]{1,0:T(8,128)(2,1)}, bf16[1792,2048]{1,0:T(8,128)(2,1)}) %tuple.74), branch_computations={%region_4.4_spmd, %region_5.5_spmd} | conditional | flops 881315840 | bytes 23740424 | solution.py:55
  167.1 4.4 fusion.25
  171.5 7.8 %convolution_convert_fusion = bf16[40,2048]{1,0:T(8,128)(2,1)S(1)} fusion(bf16[1792,2048]{1,0:T(8,128)(2,1)} %get-tuple-element.351, bf16[40,2048]{1,0:T(8,128)(2,1)S(1)} %reshape.150, bf16[2048,1792]{1,0:T(8,128)(2,1)} %get-tuple-element.350, f32[40,1792]{1,0:T(8,128)S(1)} %fusion.25), kind=kOutput, calls=%fused_computation.6 | convolution fusion | flops 587714560 | bytes 15294464 | tf_op jit(solution)/shard_map/while/body/eval_jaxpr/cond/branch_1_fun/dot_general | solution.py:45
  183.5 9.6 %all-to-all-done.1 = bf16[8,5,2048]{2,1,0:T(8,128)(2,1)S(1)} async-done(((bf16[8,5,2048]{2,1,0:T(8,128)(2,1)}), bf16[8,5,2048]{2,1,0:T(8,128)(2,1)S(1)}, u32[]{:S(2)}, u32[]{:S(2)}) %all-to-all-start.1) | async-done | bytes 163872 | tf_op jit(solution)/shard_map/while/body/eval_jaxpr/all_to_all | solution.py:56
  195.8 6.1 %collective-permute-done = bf16[3,8,2048]{2,1,0:T(8,128)(2,1)S(1)} collective-permute-done((bf16[3,8,2048]{2,1,0:T(8,128)(2,1)S(1)}, bf16[3,8,2048]{2,1,0:T(8,128)(2,1)S(1)}, u32[]{:S(2)}, u32[]{:S(2)}) %collective-permute-start) | collective-permute-done | bytes 98336 | tf_op jit(solution)/shard_map/while/body/eval_jaxpr/ppermute | solution.py:16
  208.7 9.6 %all-to-all-done = bf16[8,5,2048]{2,1,0:T(8,128)(2,1)S(1)} async-done(((bf16[8,5,2048]{2,1,0:T(8,128)(2,1)}), bf16[8,5,2048]{2,1,0:T(8,128)(2,1)S(1)}, u32[]{:S(2)}, u32[]{:S(2)}) %all-to-all-start) | async-done | bytes 163872 | tf_op jit(solution)/shard_map/while/body/eval_jaxpr/all_to_all | solution.py:54
  218.3 13.1 %conditional.2 = (bf16[8,5,2048]{2,1,0:T(8,128)(2,1)}) conditional(s32[]{:T(128)} %convert_element_type.138, () %tuple.73, (bf16[8,5,2048]{2,1,0:T(8,128)(2,1)S(1)}, bf16[2048,1792]{1,0:T(8,128)(2,1)}, bf16[2048,1792]{1,0:T(8,128)(2,1)}, bf16[1792,2048]{1,0:T(8,128)(2,1)}) %tuple.74), branch_computations={%region_4.4_spmd, %region_5.5_spmd} | conditional | flops 881315840 | bytes 23740424 | solution.py:55
  218.3 4.4 fusion.25
  222.8 7.8 %convolution_convert_fusion = bf16[40,2048]{1,0:T(8,128)(2,1)S(1)} fusion(bf16[1792,2048]{1,0:T(8,128)(2,1)} %get-tuple-element.351, bf16[40,2048]{1,0:T(8,128)(2,1)S(1)} %reshape.150, bf16[2048,1792]{1,0:T(8,128)(2,1)} %get-tuple-element.350, f32[40,1792]{1,0:T(8,128)S(1)} %fusion.25), kind=kOutput, calls=%fused_computation.6 | convolution fusion | flops 587714560 | bytes 15294464 | tf_op jit(solution)/shard_map/while/body/eval_jaxpr/cond/branch_1_fun/dot_general | solution.py:45
  234.8 9.6 %all-to-all-done.1 = bf16[8,5,2048]{2,1,0:T(8,128)(2,1)S(1)} async-done(((bf16[8,5,2048]{2,1,0:T(8,128)(2,1)}), bf16[8,5,2048]{2,1,0:T(8,128)(2,1)S(1)}, u32[]{:S(2)}, u32[]{:S(2)}) %all-to-all-start.1) | async-done | bytes 163872 | tf_op jit(solution)/shard_map/while/body/eval_jaxpr/all_to_all | solution.py:56
  247.1 6.1 %collective-permute-done = bf16[3,8,2048]{2,1,0:T(8,128)(2,1)S(1)} collective-permute-done((bf16[3,8,2048]{2,1,0:T(8,128)(2,1)S(1)}, bf16[3,8,2048]{2,1,0:T(8,128)(2,1)S(1)}, u32[]{:S(2)}, u32[]{:S(2)}) %collective-permute-start) | collective-permute-done | bytes 98336 | tf_op jit(solution)/shard_map/while/body/eval_jaxpr/ppermute | solution.py:16
  259.9 9.6 %all-to-all-done = bf16[8,5,2048]{2,1,0:T(8,128)(2,1)S(1)} async-done(((bf16[8,5,2048]{2,1,0:T(8,128)(2,1)}), bf16[8,5,2048]{2,1,0:T(8,128)(2,1)S(1)}, u32[]{:S(2)}, u32[]{:S(2)}) %all-to-all-start) | async-done | bytes 163872 | tf_op jit(solution)/shard_map/while/body/eval_jaxpr/all_to_all | solution.py:54
  269.5 13.1 %conditional.2 = (bf16[8,5,2048]{2,1,0:T(8,128)(2,1)}) conditional(s32[]{:T(128)} %convert_element_type.138, () %tuple.73, (bf16[8,5,2048]{2,1,0:T(8,128)(2,1)S(1)}, bf16[2048,1792]{1,0:T(8,128)(2,1)}, bf16[2048,1792]{1,0:T(8,128)(2,1)}, bf16[1792,2048]{1,0:T(8,128)(2,1)}) %tuple.74), branch_computations={%region_4.4_spmd, %region_5.5_spmd} | conditional | flops 881315840 | bytes 23740424 | solution.py:55
  269.6 4.4 fusion.25
  274.0 7.8 %convolution_convert_fusion = bf16[40,2048]{1,0:T(8,128)(2,1)S(1)} fusion(bf16[1792,2048]{1,0:T(8,128)(2,1)} %get-tuple-element.351, bf16[40,2048]{1,0:T(8,128)(2,1)S(1)} %reshape.150, bf16[2048,1792]{1,0:T(8,128)(2,1)} %get-tuple-element.350, f32[40,1792]{1,0:T(8,128)S(1)} %fusion.25), kind=kOutput, calls=%fused_computation.6 | convolution fusion | flops 587714560 | bytes 15294464 | tf_op jit(solution)/shard_map/while/body/eval_jaxpr/cond/branch_1_fun/dot_general | solution.py:45
  286.1 9.6 %all-to-all-done.1 = bf16[8,5,2048]{2,1,0:T(8,128)(2,1)S(1)} async-done(((bf16[8,5,2048]{2,1,0:T(8,128)(2,1)}), bf16[8,5,2048]{2,1,0:T(8,128)(2,1)S(1)}, u32[]{:S(2)}, u32[]{:S(2)}) %all-to-all-start.1) | async-done | bytes 163872 | tf_op jit(solution)/shard_map/while/body/eval_jaxpr/all_to_all | solution.py:56
  298.3 6.1 %collective-permute-done = bf16[3,8,2048]{2,1,0:T(8,128)(2,1)S(1)} collective-permute-done((bf16[3,8,2048]{2,1,0:T(8,128)(2,1)S(1)}, bf16[3,8,2048]{2,1,0:T(8,128)(2,1)S(1)}, u32[]{:S(2)}, u32[]{:S(2)}) %collective-permute-start) | collective-permute-done | bytes 98336 | tf_op jit(solution)/shard_map/while/body/eval_jaxpr/ppermute | solution.py:16
  311.2 9.6 %all-to-all-done = bf16[8,5,2048]{2,1,0:T(8,128)(2,1)S(1)} async-done(((bf16[8,5,2048]{2,1,0:T(8,128)(2,1)}), bf16[8,5,2048]{2,1,0:T(8,128)(2,1)S(1)}, u32[]{:S(2)}, u32[]{:S(2)}) %all-to-all-start) | async-done | bytes 163872 | tf_op jit(solution)/shard_map/while/body/eval_jaxpr/all_to_all | solution.py:54
  320.8 13.1 %conditional.2 = (bf16[8,5,2048]{2,1,0:T(8,128)(2,1)}) conditional(s32[]{:T(128)} %convert_element_type.138, () %tuple.73, (bf16[8,5,2048]{2,1,0:T(8,128)(2,1)S(1)}, bf16[2048,1792]{1,0:T(8,128)(2,1)}, bf16[2048,1792]{1,0:T(8,128)(2,1)}, bf16[1792,2048]{1,0:T(8,128)(2,1)}) %tuple.74), branch_computations={%region_4.4_spmd, %region_5.5_spmd} | conditional | flops 881315840 | bytes 23740424 | solution.py:55
  320.8 4.4 fusion.25
  325.3 7.8 %convolution_convert_fusion = bf16[40,2048]{1,0:T(8,128)(2,1)S(1)} fusion(bf16[1792,2048]{1,0:T(8,128)(2,1)} %get-tuple-element.351, bf16[40,2048]{1,0:T(8,128)(2,1)S(1)} %reshape.150, bf16[2048,1792]{1,0:T(8,128)(2,1)} %get-tuple-element.350, f32[40,1792]{1,0:T(8,128)S(1)} %fusion.25), kind=kOutput, calls=%fused_computation.6 | convolution fusion | flops 587714560 | bytes 15294464 | tf_op jit(solution)/shard_map/while/body/eval_jaxpr/cond/branch_1_fun/dot_general | solution.py:45
  337.3 9.6 %all-to-all-done.1 = bf16[8,5,2048]{2,1,0:T(8,128)(2,1)S(1)} async-done(((bf16[8,5,2048]{2,1,0:T(8,128)(2,1)}), bf16[8,5,2048]{2,1,0:T(8,128)(2,1)S(1)}, u32[]{:S(2)}, u32[]{:S(2)}) %all-to-all-start.1) | async-done | bytes 163872 | tf_op jit(solution)/shard_map/while/body/eval_jaxpr/all_to_all | solution.py:56
  349.6 6.1 %collective-permute-done = bf16[3,8,2048]{2,1,0:T(8,128)(2,1)S(1)} collective-permute-done((bf16[3,8,2048]{2,1,0:T(8,128)(2,1)S(1)}, bf16[3,8,2048]{2,1,0:T(8,128)(2,1)S(1)}, u32[]{:S(2)}, u32[]{:S(2)}) %collective-permute-start) | collective-permute-done | bytes 98336 | tf_op jit(solution)/shard_map/while/body/eval_jaxpr/ppermute | solution.py:16
  362.5 9.6 %all-to-all-done = bf16[8,5,2048]{2,1,0:T(8,128)(2,1)S(1)} async-done(((bf16[8,5,2048]{2,1,0:T(8,128)(2,1)}), bf16[8,5,2048]{2,1,0:T(8,128)(2,1)S(1)}, u32[]{:S(2)}, u32[]{:S(2)}) %all-to-all-start) | async-done | bytes 163872 | tf_op jit(solution)/shard_map/while/body/eval_jaxpr/all_to_all | solution.py:54
  372.0 13.1 %conditional.2 = (bf16[8,5,2048]{2,1,0:T(8,128)(2,1)}) conditional(s32[]{:T(128)} %convert_element_type.138, () %tuple.73, (bf16[8,5,2048]{2,1,0:T(8,128)(2,1)S(1)}, bf16[2048,1792]{1,0:T(8,128)(2,1)}, bf16[2048,1792]{1,0:T(8,128)(2,1)}, bf16[1792,2048]{1,0:T(8,128)(2,1)}) %tuple.74), branch_computations={%region_4.4_spmd, %region_5.5_spmd} | conditional | flops 881315840 | bytes 23740424 | solution.py:55
  372.1 4.4 fusion.25
  376.5 7.8 %convolution_convert_fusion = bf16[40,2048]{1,0:T(8,128)(2,1)S(1)} fusion(bf16[1792,2048]{1,0:T(8,128)(2,1)} %get-tuple-element.351, bf16[40,2048]{1,0:T(8,128)(2,1)S(1)} %reshape.150, bf16[2048,1792]{1,0:T(8,128)(2,1)} %get-tuple-element.350, f32[40,1792]{1,0:T(8,128)S(1)} %fusion.25), kind=kOutput, calls=%fused_computation.6 | convolution fusion | flops 587714560 | bytes 15294464 | tf_op jit(solution)/shard_map/while/body/eval_jaxpr/cond/branch_1_fun/dot_general | solution.py:45
  388.6 9.6 %all-to-all-done.1 = bf16[8,5,2048]{2,1,0:T(8,128)(2,1)S(1)} async-done(((bf16[8,5,2048]{2,1,0:T(8,128)(2,1)}), bf16[8,5,2048]{2,1,0:T(8,128)(2,1)S(1)}, u32[]{:S(2)}, u32[]{:S(2)}) %all-to-all-start.1) | async-done | bytes 163872 | tf_op jit(solution)/shard_map/while/body/eval_jaxpr/all_to_all | solution.py:56
  400.9 6.1 %collective-permute-done = bf16[3,8,2048]{2,1,0:T(8,128)(2,1)S(1)} collective-permute-done((bf16[3,8,2048]{2,1,0:T(8,128)(2,1)S(1)}, bf16[3,8,2048]{2,1,0:T(8,128)(2,1)S(1)}, u32[]{:S(2)}, u32[]{:S(2)}) %collective-permute-start) | collective-permute-done | bytes 98336 | tf_op jit(solution)/shard_map/while/body/eval_jaxpr/ppermute | solution.py:16
  413.7 9.6 %all-to-all-done = bf16[8,5,2048]{2,1,0:T(8,128)(2,1)S(1)} async-done(((bf16[8,5,2048]{2,1,0:T(8,128)(2,1)}), bf16[8,5,2048]{2,1,0:T(8,128)(2,1)S(1)}, u32[]{:S(2)}, u32[]{:S(2)}) %all-to-all-start) | async-done | bytes 163872 | tf_op jit(solution)/shard_map/while/body/eval_jaxpr/all_to_all | solution.py:54
  423.3 13.1 %conditional.2 = (bf16[8,5,2048]{2,1,0:T(8,128)(2,1)}) conditional(s32[]{:T(128)} %convert_element_type.138, () %tuple.73, (bf16[8,5,2048]{2,1,0:T(8,128)(2,1)S(1)}, bf16[2048,1792]{1,0:T(8,128)(2,1)}, bf16[2048,1792]{1,0:T(8,128)(2,1)}, bf16[1792,2048]{1,0:T(8,128)(2,1)}) %tuple.74), branch_computations={%region_4.4_spmd, %region_5.5_spmd} | conditional | flops 881315840 | bytes 23740424 | solution.py:55
  423.4 4.4 fusion.25
  427.8 7.8 %convolution_convert_fusion = bf16[40,2048]{1,0:T(8,128)(2,1)S(1)} fusion(bf16[1792,2048]{1,0:T(8,128)(2,1)} %get-tuple-element.351, bf16[40,2048]{1,0:T(8,128)(2,1)S(1)} %reshape.150, bf16[2048,1792]{1,0:T(8,128)(2,1)} %get-tuple-element.350, f32[40,1792]{1,0:T(8,128)S(1)} %fusion.25), kind=kOutput, calls=%fused_computation.6 | convolution fusion | flops 587714560 | bytes 15294464 | tf_op jit(solution)/shard_map/while/body/eval_jaxpr/cond/branch_1_fun/dot_general | solution.py:45
  439.8 9.6 %all-to-all-done.1 = bf16[8,5,2048]{2,1,0:T(8,128)(2,1)S(1)} async-done(((bf16[8,5,2048]{2,1,0:T(8,128)(2,1)}), bf16[8,5,2048]{2,1,0:T(8,128)(2,1)S(1)}, u32[]{:S(2)}, u32[]{:S(2)}) %all-to-all-start.1) | async-done | bytes 163872 | tf_op jit(solution)/shard_map/while/body/eval_jaxpr/all_to_all | solution.py:56
  452.1 6.1 %collective-permute-done = bf16[3,8,2048]{2,1,0:T(8,128)(2,1)S(1)} collective-permute-done((bf16[3,8,2048]{2,1,0:T(8,128)(2,1)S(1)}, bf16[3,8,2048]{2,1,0:T(8,128)(2,1)S(1)}, u32[]{:S(2)}, u32[]{:S(2)}) %collective-permute-start) | collective-permute-done | bytes 98336 | tf_op jit(solution)/shard_map/while/body/eval_jaxpr/ppermute | solution.py:16
  465.0 9.6 %all-to-all-done = bf16[8,5,2048]{2,1,0:T(8,128)(2,1)S(1)} async-done(((bf16[8,5,2048]{2,1,0:T(8,128)(2,1)}), bf16[8,5,2048]{2,1,0:T(8,128)(2,1)S(1)}, u32[]{:S(2)}, u32[]{:S(2)}) %all-to-all-start) | async-done | bytes 163872 | tf_op jit(solution)/shard_map/while/body/eval_jaxpr/all_to_all | solution.py:54
  474.5 13.1 %conditional.2 = (bf16[8,5,2048]{2,1,0:T(8,128)(2,1)}) conditional(s32[]{:T(128)} %convert_element_type.138, () %tuple.73, (bf16[8,5,2048]{2,1,0:T(8,128)(2,1)S(1)}, bf16[2048,1792]{1,0:T(8,128)(2,1)}, bf16[2048,1792]{1,0:T(8,128)(2,1)}, bf16[1792,2048]{1,0:T(8,128)(2,1)}) %tuple.74), branch_computations={%region_4.4_spmd, %region_5.5_spmd} | conditional | flops 881315840 | bytes 23740424 | solution.py:55
  474.6 4.4 fusion.25
  479.1 7.8 %convolution_convert_fusion = bf16[40,2048]{1,0:T(8,128)(2,1)S(1)} fusion(bf16[1792,2048]{1,0:T(8,128)(2,1)} %get-tuple-element.351, bf16[40,2048]{1,0:T(8,128)(2,1)S(1)} %reshape.150, bf16[2048,1792]{1,0:T(8,128)(2,1)} %get-tuple-element.350, f32[40,1792]{1,0:T(8,128)S(1)} %fusion.25), kind=kOutput, calls=%fused_computation.6 | convolution fusion | flops 587714560 | bytes 15294464 | tf_op jit(solution)/shard_map/while/body/eval_jaxpr/cond/branch_1_fun/dot_general | solution.py:45
  491.1 9.6 %all-to-all-done.1 = bf16[8,5,2048]{2,1,0:T(8,128)(2,1)S(1)} async-done(((bf16[8,5,2048]{2,1,0:T(8,128)(2,1)}), bf16[8,5,2048]{2,1,0:T(8,128)(2,1)S(1)}, u32[]{:S(2)}, u32[]{:S(2)}) %all-to-all-start.1) | async-done | bytes 163872 | tf_op jit(solution)/shard_map/while/body/eval_jaxpr/all_to_all | solution.py:56
  503.4 6.1 %collective-permute-done = bf16[3,8,2048]{2,1,0:T(8,128)(2,1)S(1)} collective-permute-done((bf16[3,8,2048]{2,1,0:T(8,128)(2,1)S(1)}, bf16[3,8,2048]{2,1,0:T(8,128)(2,1)S(1)}, u32[]{:S(2)}, u32[]{:S(2)}) %collective-permute-start) | collective-permute-done | bytes 98336 | tf_op jit(solution)/shard_map/while/body/eval_jaxpr/ppermute | solution.py:16
  516.2 9.6 %all-to-all-done = bf16[8,5,2048]{2,1,0:T(8,128)(2,1)S(1)} async-done(((bf16[8,5,2048]{2,1,0:T(8,128)(2,1)}), bf16[8,5,2048]{2,1,0:T(8,128)(2,1)S(1)}, u32[]{:S(2)}, u32[]{:S(2)}) %all-to-all-start) | async-done | bytes 163872 | tf_op jit(solution)/shard_map/while/body/eval_jaxpr/all_to_all | solution.py:54
  525.8 13.1 %conditional.2 = (bf16[8,5,2048]{2,1,0:T(8,128)(2,1)}) conditional(s32[]{:T(128)} %convert_element_type.138, () %tuple.73, (bf16[8,5,2048]{2,1,0:T(8,128)(2,1)S(1)}, bf16[2048,1792]{1,0:T(8,128)(2,1)}, bf16[2048,1792]{1,0:T(8,128)(2,1)}, bf16[1792,2048]{1,0:T(8,128)(2,1)}) %tuple.74), branch_computations={%region_4.4_spmd, %region_5.5_spmd} | conditional | flops 881315840 | bytes 23740424 | solution.py:55
  525.9 4.4 fusion.25
  530.3 7.8 %convolution_convert_fusion = bf16[40,2048]{1,0:T(8,128)(2,1)S(1)} fusion(bf16[1792,2048]{1,0:T(8,128)(2,1)} %get-tuple-element.351, bf16[40,2048]{1,0:T(8,128)(2,1)S(1)} %reshape.150, bf16[2048,1792]{1,0:T(8,128)(2,1)} %get-tuple-element.350, f32[40,1792]{1,0:T(8,128)S(1)} %fusion.25), kind=kOutput, calls=%fused_computation.6 | convolution fusion | flops 587714560 | bytes 15294464 | tf_op jit(solution)/shard_map/while/body/eval_jaxpr/cond/branch_1_fun/dot_general | solution.py:45
  542.3 9.6 %all-to-all-done.1 = bf16[8,5,2048]{2,1,0:T(8,128)(2,1)S(1)} async-done(((bf16[8,5,2048]{2,1,0:T(8,128)(2,1)}), bf16[8,5,2048]{2,1,0:T(8,128)(2,1)S(1)}, u32[]{:S(2)}, u32[]{:S(2)}) %all-to-all-start.1) | async-done | bytes 163872 | tf_op jit(solution)/shard_map/while/body/eval_jaxpr/all_to_all | solution.py:56
  554.6 5.2 collective-permute-done
  (305 shorter events, 133.6 us)
Async XLA Ops:
  0.0 2.1 copy-start
  5.5 14.6 %all-to-all-start = ((bf16[8,5,2048]{2,1,0:T(8,128)(2,1)}), bf16[8,5,2048]{2,1,0:T(8,128)(2,1)S(1)}, u32[]{:S(2)}, u32[]{:S(2)}) async-start(bf16[8,5,2048]{2,1,0:T(8,128)(2,1)} %bitcast.98), calls=%async_computation | async-start | bytes 524288 | tf_op jit(solution)/shard_map/while/body/eval_jaxpr/all_to_all | solution.py:54
  20.8 13.1 %all-to-all-start.1 = ((bf16[8,5,2048]{2,1,0:T(8,128)(2,1)}), bf16[8,5,2048]{2,1,0:T(8,128)(2,1)S(1)}, u32[]{:S(2)}, u32[]{:S(2)}) async-start(bf16[8,5,2048]{2,1,0:T(8,128)(2,1)} %get-tuple-element.654), calls=%async_computation.1 | async-start | bytes 524288 | tf_op jit(solution)/shard_map/while/body/eval_jaxpr/all_to_all | solution.py:56
  35.3 6.5 %collective-permute-start = (bf16[3,8,2048]{2,1,0:T(8,128)(2,1)S(1)}, bf16[3,8,2048]{2,1,0:T(8,128)(2,1)S(1)}, u32[]{:S(2)}, u32[]{:S(2)}) collective-permute-start(bf16[3,8,2048]{2,1,0:T(8,128)(2,1)S(1)} %maximum_select_fusion.2), channel_id=1, source_target_pairs={{0,8},{8,16},{16,24},{1,9},{9,17},{17,25},{2,10},{10,18},{18,26},{... | collective-permute-start | bytes 294920 | tf_op jit(solution)/shard_map/while/body/eval_jaxpr/ppermute | solution.py:16
  45.0 13.1 %all-to-all-start = ((bf16[8,5,2048]{2,1,0:T(8,128)(2,1)}), bf16[8,5,2048]{2,1,0:T(8,128)(2,1)S(1)}, u32[]{:S(2)}, u32[]{:S(2)}) async-start(bf16[8,5,2048]{2,1,0:T(8,128)(2,1)} %bitcast.98), calls=%async_computation | async-start | bytes 524288 | tf_op jit(solution)/shard_map/while/body/eval_jaxpr/all_to_all | solution.py:54
  58.8 13.1 %all-to-all-start.1 = ((bf16[8,5,2048]{2,1,0:T(8,128)(2,1)}), bf16[8,5,2048]{2,1,0:T(8,128)(2,1)S(1)}, u32[]{:S(2)}, u32[]{:S(2)}) async-start(bf16[8,5,2048]{2,1,0:T(8,128)(2,1)} %get-tuple-element.654), calls=%async_computation.1 | async-start | bytes 524288 | tf_op jit(solution)/shard_map/while/body/eval_jaxpr/all_to_all | solution.py:56
  73.3 6.5 %collective-permute-start = (bf16[3,8,2048]{2,1,0:T(8,128)(2,1)S(1)}, bf16[3,8,2048]{2,1,0:T(8,128)(2,1)S(1)}, u32[]{:S(2)}, u32[]{:S(2)}) collective-permute-start(bf16[3,8,2048]{2,1,0:T(8,128)(2,1)S(1)} %maximum_select_fusion.2), channel_id=1, source_target_pairs={{0,8},{8,16},{16,24},{1,9},{9,17},{17,25},{2,10},{10,18},{18,26},{... | collective-permute-start | bytes 294920 | tf_op jit(solution)/shard_map/while/body/eval_jaxpr/ppermute | solution.py:16
  83.0 13.1 %all-to-all-start = ((bf16[8,5,2048]{2,1,0:T(8,128)(2,1)}), bf16[8,5,2048]{2,1,0:T(8,128)(2,1)S(1)}, u32[]{:S(2)}, u32[]{:S(2)}) async-start(bf16[8,5,2048]{2,1,0:T(8,128)(2,1)} %bitcast.98), calls=%async_computation | async-start | bytes 524288 | tf_op jit(solution)/shard_map/while/body/eval_jaxpr/all_to_all | solution.py:54
  96.8 13.1 %all-to-all-start.1 = ((bf16[8,5,2048]{2,1,0:T(8,128)(2,1)}), bf16[8,5,2048]{2,1,0:T(8,128)(2,1)S(1)}, u32[]{:S(2)}, u32[]{:S(2)}) async-start(bf16[8,5,2048]{2,1,0:T(8,128)(2,1)} %get-tuple-element.654), calls=%async_computation.1 | async-start | bytes 524288 | tf_op jit(solution)/shard_map/while/body/eval_jaxpr/all_to_all | solution.py:56
  111.3 39.4 %collective-permute-start = (bf16[3,8,2048]{2,1,0:T(8,128)(2,1)S(1)}, bf16[3,8,2048]{2,1,0:T(8,128)(2,1)S(1)}, u32[]{:S(2)}, u32[]{:S(2)}) collective-permute-start(bf16[3,8,2048]{2,1,0:T(8,128)(2,1)S(1)} %maximum_select_fusion.2), channel_id=1, source_target_pairs={{0,8},{8,16},{16,24},{1,9},{9,17},{17,25},{2,10},{10,18},{18,26},{... | collective-permute-start | bytes 294920 | tf_op jit(solution)/shard_map/while/body/eval_jaxpr/ppermute | solution.py:16
  154.0 13.1 %all-to-all-start = ((bf16[8,5,2048]{2,1,0:T(8,128)(2,1)}), bf16[8,5,2048]{2,1,0:T(8,128)(2,1)S(1)}, u32[]{:S(2)}, u32[]{:S(2)}) async-start(bf16[8,5,2048]{2,1,0:T(8,128)(2,1)} %bitcast.98), calls=%async_computation | async-start | bytes 524288 | tf_op jit(solution)/shard_map/while/body/eval_jaxpr/all_to_all | solution.py:54
  180.1 13.1 %all-to-all-start.1 = ((bf16[8,5,2048]{2,1,0:T(8,128)(2,1)}), bf16[8,5,2048]{2,1,0:T(8,128)(2,1)S(1)}, u32[]{:S(2)}, u32[]{:S(2)}) async-start(bf16[8,5,2048]{2,1,0:T(8,128)(2,1)} %get-tuple-element.654), calls=%async_computation.1 | async-start | bytes 524288 | tf_op jit(solution)/shard_map/while/body/eval_jaxpr/all_to_all | solution.py:56
  194.5 7.4 %collective-permute-start = (bf16[3,8,2048]{2,1,0:T(8,128)(2,1)S(1)}, bf16[3,8,2048]{2,1,0:T(8,128)(2,1)S(1)}, u32[]{:S(2)}, u32[]{:S(2)}) collective-permute-start(bf16[3,8,2048]{2,1,0:T(8,128)(2,1)S(1)} %maximum_select_fusion.2), channel_id=1, source_target_pairs={{0,8},{8,16},{16,24},{1,9},{9,17},{17,25},{2,10},{10,18},{18,26},{... | collective-permute-start | bytes 294920 | tf_op jit(solution)/shard_map/while/body/eval_jaxpr/ppermute | solution.py:16
  205.2 13.1 %all-to-all-start = ((bf16[8,5,2048]{2,1,0:T(8,128)(2,1)}), bf16[8,5,2048]{2,1,0:T(8,128)(2,1)S(1)}, u32[]{:S(2)}, u32[]{:S(2)}) async-start(bf16[8,5,2048]{2,1,0:T(8,128)(2,1)} %bitcast.98), calls=%async_computation | async-start | bytes 524288 | tf_op jit(solution)/shard_map/while/body/eval_jaxpr/all_to_all | solution.py:54
  231.3 13.1 %all-to-all-start.1 = ((bf16[8,5,2048]{2,1,0:T(8,128)(2,1)}), bf16[8,5,2048]{2,1,0:T(8,128)(2,1)S(1)}, u32[]{:S(2)}, u32[]{:S(2)}) async-start(bf16[8,5,2048]{2,1,0:T(8,128)(2,1)} %get-tuple-element.654), calls=%async_computation.1 | async-start | bytes 524288 | tf_op jit(solution)/shard_map/while/body/eval_jaxpr/all_to_all | solution.py:56
  245.8 7.4 %collective-permute-start = (bf16[3,8,2048]{2,1,0:T(8,128)(2,1)S(1)}, bf16[3,8,2048]{2,1,0:T(8,128)(2,1)S(1)}, u32[]{:S(2)}, u32[]{:S(2)}) collective-permute-start(bf16[3,8,2048]{2,1,0:T(8,128)(2,1)S(1)} %maximum_select_fusion.2), channel_id=1, source_target_pairs={{0,8},{8,16},{16,24},{1,9},{9,17},{17,25},{2,10},{10,18},{18,26},{... | collective-permute-start | bytes 294920 | tf_op jit(solution)/shard_map/while/body/eval_jaxpr/ppermute | solution.py:16
  256.5 13.1 %all-to-all-start = ((bf16[8,5,2048]{2,1,0:T(8,128)(2,1)}), bf16[8,5,2048]{2,1,0:T(8,128)(2,1)S(1)}, u32[]{:S(2)}, u32[]{:S(2)}) async-start(bf16[8,5,2048]{2,1,0:T(8,128)(2,1)} %bitcast.98), calls=%async_computation | async-start | bytes 524288 | tf_op jit(solution)/shard_map/while/body/eval_jaxpr/all_to_all | solution.py:54
  282.6 13.1 %all-to-all-start.1 = ((bf16[8,5,2048]{2,1,0:T(8,128)(2,1)}), bf16[8,5,2048]{2,1,0:T(8,128)(2,1)S(1)}, u32[]{:S(2)}, u32[]{:S(2)}) async-start(bf16[8,5,2048]{2,1,0:T(8,128)(2,1)} %get-tuple-element.654), calls=%async_computation.1 | async-start | bytes 524288 | tf_op jit(solution)/shard_map/while/body/eval_jaxpr/all_to_all | solution.py:56
  297.0 7.4 %collective-permute-start = (bf16[3,8,2048]{2,1,0:T(8,128)(2,1)S(1)}, bf16[3,8,2048]{2,1,0:T(8,128)(2,1)S(1)}, u32[]{:S(2)}, u32[]{:S(2)}) collective-permute-start(bf16[3,8,2048]{2,1,0:T(8,128)(2,1)S(1)} %maximum_select_fusion.2), channel_id=1, source_target_pairs={{0,8},{8,16},{16,24},{1,9},{9,17},{17,25},{2,10},{10,18},{18,26},{... | collective-permute-start | bytes 294920 | tf_op jit(solution)/shard_map/while/body/eval_jaxpr/ppermute | solution.py:16
  307.7 13.1 %all-to-all-start = ((bf16[8,5,2048]{2,1,0:T(8,128)(2,1)}), bf16[8,5,2048]{2,1,0:T(8,128)(2,1)S(1)}, u32[]{:S(2)}, u32[]{:S(2)}) async-start(bf16[8,5,2048]{2,1,0:T(8,128)(2,1)} %bitcast.98), calls=%async_computation | async-start | bytes 524288 | tf_op jit(solution)/shard_map/while/body/eval_jaxpr/all_to_all | solution.py:54
  333.9 13.1 %all-to-all-start.1 = ((bf16[8,5,2048]{2,1,0:T(8,128)(2,1)}), bf16[8,5,2048]{2,1,0:T(8,128)(2,1)S(1)}, u32[]{:S(2)}, u32[]{:S(2)}) async-start(bf16[8,5,2048]{2,1,0:T(8,128)(2,1)} %get-tuple-element.654), calls=%async_computation.1 | async-start | bytes 524288 | tf_op jit(solution)/shard_map/while/body/eval_jaxpr/all_to_all | solution.py:56
  348.3 7.4 %collective-permute-start = (bf16[3,8,2048]{2,1,0:T(8,128)(2,1)S(1)}, bf16[3,8,2048]{2,1,0:T(8,128)(2,1)S(1)}, u32[]{:S(2)}, u32[]{:S(2)}) collective-permute-start(bf16[3,8,2048]{2,1,0:T(8,128)(2,1)S(1)} %maximum_select_fusion.2), channel_id=1, source_target_pairs={{0,8},{8,16},{16,24},{1,9},{9,17},{17,25},{2,10},{10,18},{18,26},{... | collective-permute-start | bytes 294920 | tf_op jit(solution)/shard_map/while/body/eval_jaxpr/ppermute | solution.py:16
  359.0 13.1 %all-to-all-start = ((bf16[8,5,2048]{2,1,0:T(8,128)(2,1)}), bf16[8,5,2048]{2,1,0:T(8,128)(2,1)S(1)}, u32[]{:S(2)}, u32[]{:S(2)}) async-start(bf16[8,5,2048]{2,1,0:T(8,128)(2,1)} %bitcast.98), calls=%async_computation | async-start | bytes 524288 | tf_op jit(solution)/shard_map/while/body/eval_jaxpr/all_to_all | solution.py:54
  385.1 13.1 %all-to-all-start.1 = ((bf16[8,5,2048]{2,1,0:T(8,128)(2,1)}), bf16[8,5,2048]{2,1,0:T(8,128)(2,1)S(1)}, u32[]{:S(2)}, u32[]{:S(2)}) async-start(bf16[8,5,2048]{2,1,0:T(8,128)(2,1)} %get-tuple-element.654), calls=%async_computation.1 | async-start | bytes 524288 | tf_op jit(solution)/shard_map/while/body/eval_jaxpr/all_to_all | solution.py:56
  399.6 7.4 %collective-permute-start = (bf16[3,8,2048]{2,1,0:T(8,128)(2,1)S(1)}, bf16[3,8,2048]{2,1,0:T(8,128)(2,1)S(1)}, u32[]{:S(2)}, u32[]{:S(2)}) collective-permute-start(bf16[3,8,2048]{2,1,0:T(8,128)(2,1)S(1)} %maximum_select_fusion.2), channel_id=1, source_target_pairs={{0,8},{8,16},{16,24},{1,9},{9,17},{17,25},{2,10},{10,18},{18,26},{... | collective-permute-start | bytes 294920 | tf_op jit(solution)/shard_map/while/body/eval_jaxpr/ppermute | solution.py:16
  410.2 13.1 %all-to-all-start = ((bf16[8,5,2048]{2,1,0:T(8,128)(2,1)}), bf16[8,5,2048]{2,1,0:T(8,128)(2,1)S(1)}, u32[]{:S(2)}, u32[]{:S(2)}) async-start(bf16[8,5,2048]{2,1,0:T(8,128)(2,1)} %bitcast.98), calls=%async_computation | async-start | bytes 524288 | tf_op jit(solution)/shard_map/while/body/eval_jaxpr/all_to_all | solution.py:54
  436.4 13.1 %all-to-all-start.1 = ((bf16[8,5,2048]{2,1,0:T(8,128)(2,1)}), bf16[8,5,2048]{2,1,0:T(8,128)(2,1)S(1)}, u32[]{:S(2)}, u32[]{:S(2)}) async-start(bf16[8,5,2048]{2,1,0:T(8,128)(2,1)} %get-tuple-element.654), calls=%async_computation.1 | async-start | bytes 524288 | tf_op jit(solution)/shard_map/while/body/eval_jaxpr/all_to_all | solution.py:56
  450.8 7.4 %collective-permute-start = (bf16[3,8,2048]{2,1,0:T(8,128)(2,1)S(1)}, bf16[3,8,2048]{2,1,0:T(8,128)(2,1)S(1)}, u32[]{:S(2)}, u32[]{:S(2)}) collective-permute-start(bf16[3,8,2048]{2,1,0:T(8,128)(2,1)S(1)} %maximum_select_fusion.2), channel_id=1, source_target_pairs={{0,8},{8,16},{16,24},{1,9},{9,17},{17,25},{2,10},{10,18},{18,26},{... | collective-permute-start | bytes 294920 | tf_op jit(solution)/shard_map/while/body/eval_jaxpr/ppermute | solution.py:16
  461.5 13.1 %all-to-all-start = ((bf16[8,5,2048]{2,1,0:T(8,128)(2,1)}), bf16[8,5,2048]{2,1,0:T(8,128)(2,1)S(1)}, u32[]{:S(2)}, u32[]{:S(2)}) async-start(bf16[8,5,2048]{2,1,0:T(8,128)(2,1)} %bitcast.98), calls=%async_computation | async-start | bytes 524288 | tf_op jit(solution)/shard_map/while/body/eval_jaxpr/all_to_all | solution.py:54
  487.6 13.1 %all-to-all-start.1 = ((bf16[8,5,2048]{2,1,0:T(8,128)(2,1)}), bf16[8,5,2048]{2,1,0:T(8,128)(2,1)S(1)}, u32[]{:S(2)}, u32[]{:S(2)}) async-start(bf16[8,5,2048]{2,1,0:T(8,128)(2,1)} %get-tuple-element.654), calls=%async_computation.1 | async-start | bytes 524288 | tf_op jit(solution)/shard_map/while/body/eval_jaxpr/all_to_all | solution.py:56
  502.1 7.4 %collective-permute-start = (bf16[3,8,2048]{2,1,0:T(8,128)(2,1)S(1)}, bf16[3,8,2048]{2,1,0:T(8,128)(2,1)S(1)}, u32[]{:S(2)}, u32[]{:S(2)}) collective-permute-start(bf16[3,8,2048]{2,1,0:T(8,128)(2,1)S(1)} %maximum_select_fusion.2), channel_id=1, source_target_pairs={{0,8},{8,16},{16,24},{1,9},{9,17},{17,25},{2,10},{10,18},{18,26},{... | collective-permute-start | bytes 294920 | tf_op jit(solution)/shard_map/while/body/eval_jaxpr/ppermute | solution.py:16
  512.7 13.1 %all-to-all-start = ((bf16[8,5,2048]{2,1,0:T(8,128)(2,1)}), bf16[8,5,2048]{2,1,0:T(8,128)(2,1)S(1)}, u32[]{:S(2)}, u32[]{:S(2)}) async-start(bf16[8,5,2048]{2,1,0:T(8,128)(2,1)} %bitcast.98), calls=%async_computation | async-start | bytes 524288 | tf_op jit(solution)/shard_map/while/body/eval_jaxpr/all_to_all | solution.py:54
  538.9 13.1 %all-to-all-start.1 = ((bf16[8,5,2048]{2,1,0:T(8,128)(2,1)}), bf16[8,5,2048]{2,1,0:T(8,128)(2,1)S(1)}, u32[]{:S(2)}, u32[]{:S(2)}) async-start(bf16[8,5,2048]{2,1,0:T(8,128)(2,1)} %get-tuple-element.654), calls=%async_computation.1 | async-start | bytes 524288 | tf_op jit(solution)/shard_map/while/body/eval_jaxpr/all_to_all | solution.py:56
  553.3 6.5 %collective-permute-start = (bf16[3,8,2048]{2,1,0:T(8,128)(2,1)S(1)}, bf16[3,8,2048]{2,1,0:T(8,128)(2,1)S(1)}, u32[]{:S(2)}, u32[]{:S(2)}) collective-permute-start(bf16[3,8,2048]{2,1,0:T(8,128)(2,1)S(1)} %maximum_select_fusion.2), channel_id=1, source_target_pairs={{0,8},{8,16},{16,24},{1,9},{9,17},{17,25},{2,10},{10,18},{18,26},{... | collective-permute-start | bytes 294920 | tf_op jit(solution)/shard_map/while/body/eval_jaxpr/ppermute | solution.py:16
  559.8 0.7 copy-start.1
where the time goes:
time: 564 us; the launch traced here: 561 us
  waiting for transfers between devices  307 us (54%)
  matrix products  97.6 us (17%)
  starting transfers between devices  90.8 us (16%)
  local copies, waits for them, and re-layouts  33.4 us (6%)
  other arithmetic  29.3 us (5%)
    all_to_all x11, waiting for transfers between devices, run_experts(): lax.all_to_all(computed, 'expert', split_axis=0, concat_axis=0, tiled=True)  106 us
    all_to_all x11, waiting for transfers between devices, run_experts(): lax.all_to_all(outgoing, 'expert', split_axis=0, concat_axis=0, tiled=True)  105 us
    ppermute x11, waiting for transfers between devices, shifted(): return lax.ppermute(value, axis, pairs)  96.5 us
    dot_general x8, matrix products, expert_rows(): jnp.dot(hidden, down_mat, preferred_element_type=jnp.float32)  62.1 us
    all_to_all x11, starting transfers between devices, run_experts(): lax.all_to_all(outgoing, 'expert', split_axis=0, concat_axis=0, tiled=True)  39 us
    all_to_all x11, starting transfers between devices, run_experts(): lax.all_to_all(computed, 'expert', split_axis=0, concat_axis=0, tiled=True)  37.5 us
    dot_general x8, matrix products, expert_rows(): gate_vals = jnp.dot(flat_rows, gate_mat, preferred_element_type=jnp.float32)  35.5 us
    ppermute x11, starting transfers between devices, shifted(): return lax.ppermute(value, axis, pairs)  14.2 us
  transfers between devices with their start and end apart: 33, of which 33 were waited for; matrix products, arithmetic and copies ran while one was open for 0% of the time, Pallas kernels for 0%

commit v1 on v0

v1 whole, which is shorter than its diff:
```python
import jax
import jax.numpy as jnp
from jax import lax
from jax.experimental import pallas as pl
from jax.experimental.pallas import tpu as pltpu
from jax.sharding import PartitionSpec as P

EXPERTS = 4


def swapped(value, axis, bit):
    pairs = [(i, i ^ bit) for i in range(lax.axis_size(axis))]
    return lax.ppermute(value, axis, pairs)


def ffn_kernel(rows_ref, gate_ref, up_ref, down_ref, keep_ref, send_ref, acc_ref):
    step = pl.program_id(0)
    rows = rows_ref[...]
    gate_vals = jnp.dot(rows, gate_ref[0], preferred_element_type=jnp.float32)
    up_vals = jnp.dot(rows, up_ref[0], preferred_element_type=jnp.float32)
    hidden = (gate_vals / (1.0 + jnp.exp(-gate_vals)) * up_vals).astype(jnp.bfloat16)
    part = jnp.dot(hidden, down_ref[0], preferred_element_type=jnp.float32)

    @pl.when(step == 0)
    def _():
        acc_ref[...] = part

    @pl.when(step > 0)
    def _():
        acc_ref[...] += part

    @pl.when(step == pl.num_programs(0) - 1)
    def _():
        half = keep_ref.shape[0]
        keep_ref[...] = acc_ref[:half, :].astype(jnp.bfloat16)
        send_ref[...] = acc_ref[half:, :].astype(jnp.bfloat16)


def ffn(rows, w_gate, w_up, w_down):
    row_count, width = rows.shape
    units = w_gate.shape[2]
    block = 256
    half = jax.ShapeDtypeStruct((row_count // 2, width), jnp.bfloat16)
    half_spec = pl.BlockSpec((row_count // 2, width), lambda i: (0, 0))
    return pl.pallas_call(
        ffn_kernel,
        out_shape=(half, half),
        grid=(units // block,),
        in_specs=[
            pl.BlockSpec((row_count, width), lambda i: (0, 0)),
            pl.BlockSpec((1, width, block), lambda i: (0, 0, i)),
            pl.BlockSpec((1, width, block), lambda i: (0, 0, i)),
            pl.BlockSpec((1, block, width), lambda i: (0, i, 0)),
        ],
        out_specs=(half_spec, half_spec),
        scratch_shapes=[pltpu.VMEM((row_count, width), jnp.float32)],
        compiler_params=pltpu.CompilerParams(dimension_semantics=("arbitrary",)),
    )(rows, w_gate, w_up, w_down)


def on_device(tokens, norm_gain, w_gate, w_up, w_down, expert_ids, slot_ids, dropped, gate_weights):
    groups = lax.axis_size("expert")
    sections = lax.axis_size("section")
    section_at = lax.axis_index("section")
    expert_at = lax.axis_index("expert")
    local_count = EXPERTS // 2
    shards = groups // local_count
    micro_count, tok_rows, width = tokens.shape
    capacity = 5 * tok_rows // (2 * EXPERTS)
    layers = sections // 2
    layer_at = section_at // 2
    half_at = section_at % 2
    group_at = expert_at // shards
    gain_row = lax.dynamic_index_in_dim(norm_gain, layer_at, 0, keepdims=False)
    route = lax.dynamic_index_in_dim(expert_ids, layer_at, 0, keepdims=False)
    slot = lax.dynamic_index_in_dim(slot_ids, layer_at, 0, keepdims=False)
    drop = lax.dynamic_index_in_dim(dropped, layer_at, 0, keepdims=False)
    weigh = lax.dynamic_index_in_dim(gate_weights, layer_at, 0, keepdims=False)

    tok_total = micro_count * tok_rows
    slot_total = micro_count * capacity
    local_id = route - half_at * local_count
    owned = (drop == 0) & (local_id >= 0) & (local_id < local_count)
    relative = local_id ^ group_at
    micro_of = jnp.arange(micro_count, dtype=jnp.int32)[:, None, None]
    place = relative * slot_total + micro_of * capacity + slot
    place = jnp.where(owned, place, -1).reshape(tok_total, 2)
    columns = jnp.arange(local_count * slot_total, dtype=jnp.int32)[None, :]
    weights = weigh.reshape(tok_total, 2)
    hit_first = place[:, 0:1] == columns
    hit_second = place[:, 1:2] == columns
    mix = jnp.where(hit_first, weights[:, 0:1], 0.0) + jnp.where(hit_second, weights[:, 1:2], 0.0)
    mix_high = mix.astype(jnp.bfloat16)
    mix_low = (mix - mix_high.astype(jnp.float32)).astype(jnp.bfloat16)
    pick = (hit_first | hit_second).astype(jnp.bfloat16).T

    bits = []
    bit = shards // 2
    while bit:
        bits.append(bit)
        bit //= 2

    state = tokens.reshape(tok_total, width)
    result = jnp.zeros((tok_total, width), jnp.bfloat16)
    for layer in range(layers):
        wide = state.astype(jnp.float32)
        inv_scale = lax.rsqrt(jnp.mean(wide * wide, axis=-1, keepdims=True) + 1e-05)
        normed = (wide * inv_scale * gain_row).astype(jnp.bfloat16)
        own = jnp.dot(pick[:slot_total], normed, preferred_element_type=jnp.float32)
        away = jnp.dot(pick[slot_total:], normed, preferred_element_type=jnp.float32)
        come = swapped(away.astype(jnp.bfloat16), "expert", shards)
        rows = jnp.concatenate([own.astype(jnp.bfloat16), come])
        for bit in bits:
            rows = jnp.concatenate([rows, swapped(rows, "expert", bit)])
        keep, send = ffn(rows, w_gate, w_up, w_down)
        for bit in bits[::-1]:
            back = swapped(send, "expert", bit)
            total = (keep.astype(jnp.float32) + back.astype(jnp.float32)).astype(jnp.bfloat16)
            keep, send = total[: total.shape[0] // 2], total[total.shape[0] // 2 :]
        back = swapped(send, "expert", shards)
        produced = jnp.concatenate([keep, back])
        part = jnp.dot(mix_high, produced, preferred_element_type=jnp.float32) + jnp.dot(
            mix_low, produced, preferred_element_type=jnp.float32
        )
        other = swapped(part.astype(jnp.bfloat16), "section", 1).astype(jnp.float32)
        both = (wide + part + other).astype(jnp.bfloat16)
        shown = jnp.where(half_at == 0, (wide + part).astype(jnp.bfloat16), both)
        result = jnp.where(layer_at == layer, shown, result)
        if layer + 1 < layers:
            state = lax.ppermute(both, "section", [(i, i + 2) for i in range(sections - 2)])
    return result.reshape(1, micro_count, tok_rows, width)


def solution(mesh):
    return jax.shard_map(
        on_device,
        mesh=mesh,
        in_specs=(
            P(None, "expert", None),
            P(),
            P("section", None, "expert"),
            P("section", None, "expert"),
            P("section", "expert", None),
            P(None, None, "expert", None),
            P(None, None, "expert", None),
            P(None, None, "expert", None),
            P(None, None, "expert", None),
        ),
        out_specs=P("section", None, "expert", None),
        check_vma=False,
    )
```

time: 564 us -> 153 us (0.27)
  waiting for transfers between devices: 307 us -> 94.5 us
  matrix products: 97.6 us -> 4.1 us
  starting transfers between devices: 90.8 us -> 12.7 us
  local copies, waits for them, and re-layouts: 33.4 us -> 0.72 us
  Pallas kernels: 0 us -> 31.1 us
  other arithmetic: 29.3 us -> 8.94 us
    all_to_all x22 -> x0, waiting for transfers between devices: 211 us -> none  [the longest x11 106 us: run_experts(): lax.all_to_all(computed, 'expert', split_axis=0, concat_axis=0, tiled=True)]
    dot_general x16 -> x8, matrix products: 97.6 us -> 4.1 us  [the longest x2 1.48 us: on_device(): jnp.dot(pick[slot_total:], normed, preferred_element_type=jnp.float32)]
    all_to_all x22 -> x0, starting transfers between devices: 76.5 us -> none  [the longest x11 39 us: run_experts(): lax.all_to_all(outgoing, 'expert', split_axis=0, concat_axis=0, tiled=True)]
    pallas_call x0 -> x2, Pallas kernels: none -> 31.1 us  [ffn(): pl.pallas_call(ffn_kernel, out_shape=(half, half), grid=(units // block,)...]
    scatter x22 -> x0, other arithmetic: 16.9 us -> none  [the longest x11 8.7 us: advance(): buffer = buffer.at[target[:, 1]].set(normed, mode='drop')]
    gather x22 -> x0, local copies, waits for them, and re-layouts: 12.7 us -> none  [advance(): own_rows = flat_back[clipped[:, member]]]
    reduce_sum x22 -> x2, other arithmetic: 10.4 us -> 1.24 us  [on_device(): inv_scale = lax.rsqrt(jnp.mean(wide * wide, axis=-1, keepdims=True) + 1e-05)]
    broadcast_in_dim x24 -> x1, local copies, waits for them, and re-layouts: 8.04 us -> 0.01 us  [on_device(): jnp.where(hit_first, weights[:, 0:1], 0.0)]
  transfers between devices with their start and end apart: 33 -> 15, of which waited for: 33 -> 15; matrix products, arithmetic and copies ran while one was open for 0% -> 1% of each run, Pallas kernels for 0% -> 0%
where the time goes in v1:
time: 153 us; the launch traced here: 152 us
  waiting for transfers between devices  94.5 us (62%)
  Pallas kernels  31.1 us (20%)
  starting transfers between devices  12.7 us (8%)
  other arithmetic  8.94 us (6%)
  matrix products  4.1 us (3%)
    ppermute x14, waiting for transfers between devices, swapped(): return lax.ppermute(value, axis, pairs)  87.5 us
    pallas_call x2, Pallas kernels, ffn(): pl.pallas_call(ffn_kernel, out_shape=(half, half), grid=(units // block,)...  31.1 us
    ppermute x14, starting transfers between devices, swapped(): return lax.ppermute(value, axis, pairs)  11.4 us
    ppermute x1, waiting for transfers between devices, on_device(): lax.ppermute(both, 'section', [(i, i + 2) for i in range(sections - 2)])  6.97 us
  transfers between devices with their start and end apart: 15, of which 15 were waited for; matrix products, arithmetic and copies ran while one was open for 1% of the time, Pallas kernels for 0%

profile of v1, /device:TPU:6, one launch (start us, length us, event | category | flops | bytes accessed | tf_op | source)
XLA Modules:
  0.0 152.3 jit_solution(3346121809884870443)
XLA Ops:
  0.0 0.0 copy-start
  0.0 0.7 xor_multiply_fusion
  0.7 0.1 mul.63
  0.8 0.1 squeeze.10
  0.9 0.7 compare_and_fusion
  1.7 0.1 and.32
  1.7 0.1 add.87
  1.8 0.1 add.88
  1.9 0.0 copy-done
  1.9 1.1 fusion.4
  3.0 0.1 rsqrt.20
  3.2 1.2 convolution_convert_fusion.2
  4.4 2.7 %collective-permute-start = (bf16[40,2048]{1,0:T(8,128)(2,1)S(1)}, bf16[40,2048]{1,0:T(8,128)(2,1)S(1)}, u32[]{:S(2)}, u32[]{:S(2)}) collective-permute-start(bf16[40,2048]{1,0:T(8,128)(2,1)S(1)} %convolution_convert_fusion.2), channel_id=1, source_target_pairs={{0,4},{1,5},{2,6},{3,7},{4,0},{5,1},{6,2},{7,3},{8,12},{9,13},{10,... | collective-permute-start | bytes 491528 | tf_op jit(solution)/shard_map/ppermute | solution.py:13
  7.0 1.2 convolution_convert_fusion.3
  8.2 6.5 %collective-permute-done = bf16[40,2048]{1,0:T(8,128)(2,1)S(1)} collective-permute-done((bf16[40,2048]{1,0:T(8,128)(2,1)S(1)}, bf16[40,2048]{1,0:T(8,128)(2,1)S(1)}, u32[]{:S(2)}, u32[]{:S(2)}) %collective-permute-start) | collective-permute-done | bytes 163872 | tf_op jit(solution)/shard_map/ppermute | solution.py:13
  14.8 0.7 collective-permute-start.1
  15.5 7.9 %collective-permute-done.1 = bf16[80,2048]{1,0:T(8,128)(2,1)S(1)} collective-permute-done((bf16[80,2048]{1,0:T(8,128)(2,1)S(1)}, bf16[80,2048]{1,0:T(8,128)(2,1)S(1)}, u32[]{:S(2)}, u32[]{:S(2)}) %collective-permute-start.1) | collective-permute-done | bytes 327712 | tf_op jit(solution)/shard_map/ppermute | solution.py:13
  23.5 0.1 collective-permute-start.2
  23.6 2.1 %collective-permute-done.2 = bf16[160,2048]{1,0:T(8,128)(2,1)S(1)} collective-permute-done((bf16[160,2048]{1,0:T(8,128)(2,1)S(1)}, bf16[160,2048]{1,0:T(8,128)(2,1)S(1)}, u32[]{:S(2)}, u32[]{:S(2)}) %collective-permute-start.2) | collective-permute-done | bytes 655392 | tf_op jit(solution)/shard_map/ppermute | solution.py:13
  25.7 1.2 pad_maximum_fusion.rows_ref
  26.9 15.6 %shard_map.91 = (bf16[160,2048]{1,0:T(8,128)(2,1)}, bf16[160,2048]{1,0:T(8,128)(2,1)}) custom-call(bf16[320,2048]{1,0:T(8,128)(2,1)} %pad_maximum_fusion.rows_ref, bf16[1,2048,1792]{2,1,0:T(8,128)(2,1)} %gate_ref.3, bf16[1,2048,1792]{2,1,0:T(8,128)(2,1)} %up_ref.3, bf16[1,1792,2048]{2,1,0:T(8,128)(2,1)} %down_ref.3), custom_call_target="tpu_custom_call" | custom-call | tf_op jit(solution)/shard_map/pallas_call | solution.py:45
  42.4 0.1 collective-permute-start.3
  42.6 2.2 %collective-permute-done.3 = bf16[160,2048]{1,0:T(8,128)(2,1)S(1)} collective-permute-done((bf16[160,2048]{1,0:T(8,128)(2,1)}, bf16[160,2048]{1,0:T(8,128)(2,1)S(1)}, u32[]{:S(2)}, u32[]{:S(2)}) %collective-permute-start.3) | collective-permute-done | bytes 655392 | tf_op jit(solution)/shard_map/ppermute | solution.py:13
  44.7 1.3 add_convert_fusion.1
  46.1 1.8 %collective-permute-start.4 = (bf16[80,2048]{1,0:T(8,128)(2,1)S(1)}, bf16[80,2048]{1,0:T(8,128)(2,1)S(1)}, u32[]{:S(2)}, u32[]{:S(2)}) collective-permute-start(bf16[80,2048]{1,0:T(8,128)(2,1)S(1)} %slice.61), channel_id=1, source_target_pairs={{0,2},{1,3},{2,0},{3,1},{4,6},{5,7},{6,4},{7,5},{8,10},{9,11},{10,... | collective-permute-start | bytes 983048 | tf_op jit(solution)/shard_map/ppermute | solution.py:13
  47.8 0.0 copy-done.2
  47.8 0.1 reshape.59
  47.9 8.0 %collective-permute-done.4 = bf16[80,2048]{1,0:T(8,128)(2,1)S(1)} collective-permute-done((bf16[80,2048]{1,0:T(8,128)(2,1)S(1)}, bf16[80,2048]{1,0:T(8,128)(2,1)S(1)}, u32[]{:S(2)}, u32[]{:S(2)}) %collective-permute-start.4) | collective-permute-done | bytes 327712 | tf_op jit(solution)/shard_map/ppermute | solution.py:13
  55.9 0.1 add_convert_fusion.3
  56.0 0.0 copy-start.1
  56.0 3.4 %collective-permute-start.5 = (bf16[40,2048]{1,0:T(8,128)(2,1)S(1)}, bf16[40,2048]{1,0:T(8,128)(2,1)S(1)}, u32[]{:S(2)}, u32[]{:S(2)}) collective-permute-start(bf16[40,2048]{1,0:T(8,128)(2,1)S(1)} %get-tuple-element.16), channel_id=1, source_target_pairs={{0,4},{1,5},{2,6},{3,7},{4,0},{5,1},{6,2},{7,3},{8,12},{9,13},{10,... | collective-permute-start | bytes 491528 | tf_op jit(solution)/shard_map/ppermute | solution.py:13
  59.4 7.2 %collective-permute-done.5 = bf16[40,2048]{1,0:T(8,128)(2,1)S(1)} collective-permute-done((bf16[40,2048]{1,0:T(8,128)(2,1)S(1)}, bf16[40,2048]{1,0:T(8,128)(2,1)S(1)}, u32[]{:S(2)}, u32[]{:S(2)}) %collective-permute-start.5) | collective-permute-done | bytes 163872 | tf_op jit(solution)/shard_map/ppermute | solution.py:13
  66.6 0.3 fusion.16
  66.9 0.3 fusion.39
  67.2 0.6 collective-permute-start.6
  67.8 6.5 %collective-permute-done.6 = bf16[64,2048]{1,0:T(8,128)(2,1)S(1)} collective-permute-done((bf16[64,2048]{1,0:T(8,128)(2,1)S(1)}, bf16[64,2048]{1,0:T(8,128)(2,1)S(1)}, u32[]{:S(2)}, u32[]{:S(2)}) %collective-permute-start.6) | collective-permute-done | bytes 262176 | tf_op jit(solution)/shard_map/ppermute | solution.py:13
  74.3 0.0 copy-done.1
  74.3 0.1 add_convert_fusion.5
  74.4 1.3 collective-permute-start.7
  75.7 7.0 %collective-permute-done.7 = bf16[64,2048]{1,0:T(8,128)(2,1)S(1)} collective-permute-done((bf16[64,2048]{1,0:T(8,128)(2,1)S(1)}, bf16[64,2048]{1,0:T(8,128)(2,1)S(1)}, u32[]{:S(2)}, u32[]{:S(2)}) %collective-permute-start.7) | collective-permute-done | bytes 262176 | tf_op jit(solution)/shard_map/ppermute | solution.py:130
  82.6 0.2 fusion.5
  82.8 0.3 convolution_convert_fusion
  83.1 0.1 collective-permute-start.8
  83.2 0.3 convolution_convert_fusion.1
  83.4 9.5 %collective-permute-done.8 = bf16[40,2048]{1,0:T(8,128)(2,1)S(1)} collective-permute-done((bf16[40,2048]{1,0:T(8,128)(2,1)S(1)}, bf16[40,2048]{1,0:T(8,128)(2,1)S(1)}, u32[]{:S(2)}, u32[]{:S(2)}) %collective-permute-start.8) | collective-permute-done | bytes 163872 | tf_op jit(solution)/shard_map/ppermute | solution.py:13
  93.0 0.1 collective-permute-start.9
  93.1 7.1 %collective-permute-done.9 = bf16[80,2048]{1,0:T(8,128)(2,1)S(1)} collective-permute-done((bf16[80,2048]{1,0:T(8,128)(2,1)S(1)}, bf16[80,2048]{1,0:T(8,128)(2,1)S(1)}, u32[]{:S(2)}, u32[]{:S(2)}) %collective-permute-start.9) | collective-permute-done | bytes 327712 | tf_op jit(solution)/shard_map/ppermute | solution.py:13
  100.2 0.1 collective-permute-start.10
  100.3 2.1 %collective-permute-done.10 = bf16[160,2048]{1,0:T(8,128)(2,1)S(1)} collective-permute-done((bf16[160,2048]{1,0:T(8,128)(2,1)S(1)}, bf16[160,2048]{1,0:T(8,128)(2,1)S(1)}, u32[]{:S(2)}, u32[]{:S(2)}) %collective-permute-start.10) | collective-permute-done | bytes 655392 | tf_op jit(solution)/shard_map/ppermute | solution.py:13
  102.4 1.2 pad_maximum_fusion.1.rows_ref
  103.5 15.5 %shard_map.92 = (bf16[160,2048]{1,0:T(8,128)(2,1)}, bf16[160,2048]{1,0:T(8,128)(2,1)}) custom-call(bf16[320,2048]{1,0:T(8,128)(2,1)} %pad_maximum_fusion.1.rows_ref, bf16[1,2048,1792]{2,1,0:T(8,128)(2,1)} %gate_ref.3, bf16[1,2048,1792]{2,1,0:T(8,128)(2,1)} %up_ref.3, bf16[1,1792,2048]{2,1,0:T(8,128)(2,1)} %down_ref.3), custom_call_target="tpu_custom_call" | custom-call | tf_op jit(solution)/shard_map/pallas_call | solution.py:45
  119.1 0.1 collective-permute-start.11
  119.2 2.2 %collective-permute-done.11 = bf16[160,2048]{1,0:T(8,128)(2,1)S(1)} collective-permute-done((bf16[160,2048]{1,0:T(8,128)(2,1)}, bf16[160,2048]{1,0:T(8,128)(2,1)S(1)}, u32[]{:S(2)}, u32[]{:S(2)}) %collective-permute-start.11) | collective-permute-done | bytes 655392 | tf_op jit(solution)/shard_map/ppermute | solution.py:13
  121.4 1.3 add_convert_fusion
  122.7 0.1 collective-permute-start.12
  122.8 9.7 %collective-permute-done.12 = bf16[80,2048]{1,0:T(8,128)(2,1)S(1)} collective-permute-done((bf16[80,2048]{1,0:T(8,128)(2,1)S(1)}, bf16[80,2048]{1,0:T(8,128)(2,1)S(1)}, u32[]{:S(2)}, u32[]{:S(2)}) %collective-permute-start.12) | collective-permute-done | bytes 327712 | tf_op jit(solution)/shard_map/ppermute | solution.py:13
  132.5 0.1 add_convert_fusion.2
  132.6 1.0 collective-permute-start.13
  133.7 8.8 %collective-permute-done.13 = bf16[40,2048]{1,0:T(8,128)(2,1)S(1)} collective-permute-done((bf16[40,2048]{1,0:T(8,128)(2,1)S(1)}, bf16[40,2048]{1,0:T(8,128)(2,1)S(1)}, u32[]{:S(2)}, u32[]{:S(2)}) %collective-permute-start.13) | collective-permute-done | bytes 163872 | tf_op jit(solution)/shard_map/ppermute | solution.py:13
  142.5 0.3 fusion.15
  142.8 0.3 fusion.40
  143.1 0.6 collective-permute-start.14
  143.7 7.7 %collective-permute-done.14 = bf16[64,2048]{1,0:T(8,128)(2,1)S(1)} collective-permute-done((bf16[64,2048]{1,0:T(8,128)(2,1)S(1)}, bf16[64,2048]{1,0:T(8,128)(2,1)S(1)}, u32[]{:S(2)}, u32[]{:S(2)}) %collective-permute-start.14) | collective-permute-done | bytes 262176 | tf_op jit(solution)/shard_map/ppermute | solution.py:13
  151.4 0.9 fusion.12
  (22 shorter events, 0.3 us)
Async XLA Ops:
  0.0 1.9 %copy-start = (f32[2,2048]{1,0:T(2,128)S(1)}, f32[2,2048]{1,0:T(2,128)}, u32[]{:S(2)}) copy-start(f32[2,2048]{1,0:T(2,128)} %param.10) | copy-start | bytes 49156
  4.4 10.4 %collective-permute-start = (bf16[40,2048]{1,0:T(8,128)(2,1)S(1)}, bf16[40,2048]{1,0:T(8,128)(2,1)S(1)}, u32[]{:S(2)}, u32[]{:S(2)}) collective-permute-start(bf16[40,2048]{1,0:T(8,128)(2,1)S(1)} %convolution_convert_fusion.2), channel_id=1, source_target_pairs={{0,4},{1,5},{2,6},{3,7},{4,0},{5,1},{6,2},{7,3},{8,12},{9,13},{10,... | collective-permute-start | bytes 491528 | tf_op jit(solution)/shard_map/ppermute | solution.py:13
  14.8 8.7 %collective-permute-start.1 = (bf16[80,2048]{1,0:T(8,128)(2,1)S(1)}, bf16[80,2048]{1,0:T(8,128)(2,1)S(1)}, u32[]{:S(2)}, u32[]{:S(2)}) collective-permute-start(bf16[80,2048]{1,0:T(8,128)(2,1)S(1)} %pad_maximum_fusion.4), channel_id=1, source_target_pairs={{0,2},{1,3},{2,0},{3,1},{4,6},{5,7},{6,4},{7,5},{8,10},{9,11},{10,... | collective-permute-start | bytes 983048 | tf_op jit(solution)/shard_map/ppermute | solution.py:13
  23.5 2.2 %collective-permute-start.2 = (bf16[160,2048]{1,0:T(8,128)(2,1)S(1)}, bf16[160,2048]{1,0:T(8,128)(2,1)S(1)}, u32[]{:S(2)}, u32[]{:S(2)}) collective-permute-start(bf16[160,2048]{1,0:T(8,128)(2,1)S(1)} %pad_maximum_fusion.2), channel_id=1, source_target_pairs={{0,1},{1,0},{2,3},{3,2},{4,5},{5,4},{6,7},{7,6},{8,9},{9,8},{10,11... | collective-permute-start | bytes 1966088 | tf_op jit(solution)/shard_map/ppermute | solution.py:13
  42.4 2.3 %collective-permute-start.3 = (bf16[160,2048]{1,0:T(8,128)(2,1)}, bf16[160,2048]{1,0:T(8,128)(2,1)S(1)}, u32[]{:S(2)}, u32[]{:S(2)}) collective-permute-start(bf16[160,2048]{1,0:T(8,128)(2,1)} %get-tuple-element.10), channel_id=1, source_target_pairs={{0,1},{1,0},{2,3},{3,2},{4,5},{5,4},{6,7},{7,6},{8,9},{9,8},{10,11... | collective-permute-start | bytes 1966088 | tf_op jit(solution)/shard_map/ppermute | solution.py:13
  44.7 3.1 %copy-start.2 = (f32[2,8,8,2]{2,3,1,0:T(2,128)S(1)}, f32[2,8,8,2]{2,3,1,0:T(2,128)}, u32[]{:S(2)}) copy-start(f32[2,8,8,2]{2,3,1,0:T(2,128)} %param.17) | copy-start | bytes 3076
  46.1 9.8 %collective-permute-start.4 = (bf16[80,2048]{1,0:T(8,128)(2,1)S(1)}, bf16[80,2048]{1,0:T(8,128)(2,1)S(1)}, u32[]{:S(2)}, u32[]{:S(2)}) collective-permute-start(bf16[80,2048]{1,0:T(8,128)(2,1)S(1)} %slice.61), channel_id=1, source_target_pairs={{0,2},{1,3},{2,0},{3,1},{4,6},{5,7},{6,4},{7,5},{8,10},{9,11},{10,... | collective-permute-start | bytes 983048 | tf_op jit(solution)/shard_map/ppermute | solution.py:13
  56.0 18.3 %copy-start.1 = (bf16[8,8,2048]{2,1,0:T(8,128)(2,1)S(1)}, bf16[8,8,2048]{2,1,0:T(8,128)(2,1)}, u32[]{:S(2)}) copy-start(bf16[8,8,2048]{2,1,0:T(8,128)(2,1)} %param.9) | copy-start | bytes 786436
  56.0 10.6 %collective-permute-start.5 = (bf16[40,2048]{1,0:T(8,128)(2,1)S(1)}, bf16[40,2048]{1,0:T(8,128)(2,1)S(1)}, u32[]{:S(2)}, u32[]{:S(2)}) collective-permute-start(bf16[40,2048]{1,0:T(8,128)(2,1)S(1)} %get-tuple-element.16), channel_id=1, source_target_pairs={{0,4},{1,5},{2,6},{3,7},{4,0},{5,1},{6,2},{7,3},{8,12},{9,13},{10,... | collective-permute-start | bytes 491528 | tf_op jit(solution)/shard_map/ppermute | solution.py:13
  67.2 7.1 %collective-permute-start.6 = (bf16[64,2048]{1,0:T(8,128)(2,1)S(1)}, bf16[64,2048]{1,0:T(8,128)(2,1)S(1)}, u32[]{:S(2)}, u32[]{:S(2)}) collective-permute-start(bf16[64,2048]{1,0:T(8,128)(2,1)S(1)} %get-tuple-element.21), channel_id=1, source_target_pairs={{0,8},{8,0},{16,24},{24,16},{1,9},{9,1},{17,25},{25,17},{2,10},{10... | collective-permute-start | bytes 786440 | tf_op jit(solution)/shard_map/ppermute | solution.py:13
  74.4 8.3 %collective-permute-start.7 = (bf16[64,2048]{1,0:T(8,128)(2,1)S(1)}, bf16[64,2048]{1,0:T(8,128)(2,1)S(1)}, u32[]{:S(2)}, u32[]{:S(2)}) collective-permute-start(bf16[64,2048]{1,0:T(8,128)(2,1)S(1)} %add_convert_fusion.5), channel_id=1, source_target_pairs={{0,16},{8,24},{1,17},{9,25},{2,18},{10,26},{3,19},{11,27},{4,20},{... | collective-permute-start | bytes 786440 | tf_op jit(solution)/shard_map/ppermute | solution.py:130
  83.1 9.9 %collective-permute-start.8 = (bf16[40,2048]{1,0:T(8,128)(2,1)S(1)}, bf16[40,2048]{1,0:T(8,128)(2,1)S(1)}, u32[]{:S(2)}, u32[]{:S(2)}) collective-permute-start(bf16[40,2048]{1,0:T(8,128)(2,1)S(1)} %convolution_convert_fusion), channel_id=1, source_target_pairs={{0,4},{1,5},{2,6},{3,7},{4,0},{5,1},{6,2},{7,3},{8,12},{9,13},{10,... | collective-permute-start | bytes 491528 | tf_op jit(solution)/shard_map/ppermute | solution.py:13
  93.0 7.1 %collective-permute-start.9 = (bf16[80,2048]{1,0:T(8,128)(2,1)S(1)}, bf16[80,2048]{1,0:T(8,128)(2,1)S(1)}, u32[]{:S(2)}, u32[]{:S(2)}) collective-permute-start(bf16[80,2048]{1,0:T(8,128)(2,1)S(1)} %pad_maximum_fusion.6), channel_id=1, source_target_pairs={{0,2},{1,3},{2,0},{3,1},{4,6},{5,7},{6,4},{7,5},{8,10},{9,11},{10,... | collective-permute-start | bytes 983048 | tf_op jit(solution)/shard_map/ppermute | solution.py:13
  100.2 2.2 %collective-permute-start.10 = (bf16[160,2048]{1,0:T(8,128)(2,1)S(1)}, bf16[160,2048]{1,0:T(8,128)(2,1)S(1)}, u32[]{:S(2)}, u32[]{:S(2)}) collective-permute-start(bf16[160,2048]{1,0:T(8,128)(2,1)S(1)} %pad_maximum_fusion.3), channel_id=1, source_target_pairs={{0,1},{1,0},{2,3},{3,2},{4,5},{5,4},{6,7},{7,6},{8,9},{9,8},{10,11... | collective-permute-start | bytes 1966088 | tf_op jit(solution)/shard_map/ppermute | solution.py:13
  119.1 2.3 %collective-permute-start.11 = (bf16[160,2048]{1,0:T(8,128)(2,1)}, bf16[160,2048]{1,0:T(8,128)(2,1)S(1)}, u32[]{:S(2)}, u32[]{:S(2)}) collective-permute-start(bf16[160,2048]{1,0:T(8,128)(2,1)} %get-tuple-element.12), channel_id=1, source_target_pairs={{0,1},{1,0},{2,3},{3,2},{4,5},{5,4},{6,7},{7,6},{8,9},{9,8},{10,11... | collective-permute-start | bytes 1966088 | tf_op jit(solution)/shard_map/ppermute | solution.py:13
  122.7 9.8 %collective-permute-start.12 = (bf16[80,2048]{1,0:T(8,128)(2,1)S(1)}, bf16[80,2048]{1,0:T(8,128)(2,1)S(1)}, u32[]{:S(2)}, u32[]{:S(2)}) collective-permute-start(bf16[80,2048]{1,0:T(8,128)(2,1)S(1)} %slice.65), channel_id=1, source_target_pairs={{0,2},{1,3},{2,0},{3,1},{4,6},{5,7},{6,4},{7,5},{8,10},{9,11},{10,... | collective-permute-start | bytes 983048 | tf_op jit(solution)/shard_map/ppermute | solution.py:13
  132.6 9.9 %collective-permute-start.13 = (bf16[40,2048]{1,0:T(8,128)(2,1)S(1)}, bf16[40,2048]{1,0:T(8,128)(2,1)S(1)}, u32[]{:S(2)}, u32[]{:S(2)}) collective-permute-start(bf16[40,2048]{1,0:T(8,128)(2,1)S(1)} %get-tuple-element.14), channel_id=1, source_target_pairs={{0,4},{1,5},{2,6},{3,7},{4,0},{5,1},{6,2},{7,3},{8,12},{9,13},{10,... | collective-permute-start | bytes 491528 | tf_op jit(solution)/shard_map/ppermute | solution.py:13
  143.1 8.3 %collective-permute-start.14 = (bf16[64,2048]{1,0:T(8,128)(2,1)S(1)}, bf16[64,2048]{1,0:T(8,128)(2,1)S(1)}, u32[]{:S(2)}, u32[]{:S(2)}) collective-permute-start(bf16[64,2048]{1,0:T(8,128)(2,1)S(1)} %get-tuple-element.23), channel_id=1, source_target_pairs={{0,8},{8,0},{16,24},{24,16},{1,9},{9,1},{17,25},{25,17},{2,10},{10... | collective-permute-start | bytes 786440 | tf_op jit(solution)/shard_map/ppermute | solution.py:13
